TPU v7x, 32 devices: a whole 2x2x4 slice. The times are simulated.
32 devices in a mesh: cohort: 2 (over x), tile: 16 (over z, y, core).
Axes of the slice: x: 2, y: 2, z: 4, core: 2. Of those that a mesh axis runs over, the one named last changes fastest.
Arguments:
- dosage: bfloat16 [512, 8192], P(('cohort', 'tile')), parts along dimension 0, may hold values from 0 to 2
- covars: float32 [512, 16], P(('cohort', 'tile')), parts along dimension 0, may hold values from -12 to 12, as said below
- phenotypes: float32 [512, 1792], P(('cohort', 'tile')), parts along dimension 0, may hold values from -100 to 100
Outputs:
- mean_chi: float32 [3584], P(('cohort', 'tile')), parts along dimension 0
- hit_rate: float32 [3584], P(('cohort', 'tile')), parts along dimension 0
There are 2 independent parts, one for each index of `cohort`. A program takes and returns all parts, laid end to end along the dimension named above; each array names one. Nothing has to cross between parts.
Inputs may be any that keep to these rules, and one draw needn't show every extreme that they name: `covars`: each covariate column has its own mean and spread.
All inputs are finite; a program needn't handle non-finite values.
Results may differ from a plain program's by a relative error of at most 0.003.
Values may be sent and summed in bfloat16 or wider, within the bound.
A program may use at most 64 MiB of HBM per device.

v0:
```python
import jax
import jax.numpy as jnp
from jax import lax
from jax.sharding import PartitionSpec as P


def local(dosage, covars, phenotypes):
    highest = lax.Precision.HIGHEST
    devices = lax.axis_size("tile")
    local_rows = dosage.shape[0]
    variants = dosage.shape[1]
    samples = local_rows * devices
    genes_all = phenotypes.shape[1]
    gene_own = genes_all // devices
    scale_root = jnp.sqrt(jnp.float32(samples))
    covars_all = lax.all_gather(covars, "tile", axis=0, tiled=True)
    dose_all = lax.all_gather(dosage, "tile", axis=0, tiled=True)
    pheno_own = lax.all_to_all(phenotypes, "tile", split_axis=1, concat_axis=0, tiled=True)
    gram = jnp.dot(covars_all.T, covars_all, precision=highest, preferred_element_type=jnp.float32)
    factor = jnp.linalg.cholesky(gram)
    cov_pheno = jnp.dot(
        covars_all.T, pheno_own, precision=highest, preferred_element_type=jnp.float32
    )
    beta_pheno = jax.scipy.linalg.cho_solve((factor, True), cov_pheno)
    pheno_resid = pheno_own - jnp.dot(
        covars_all, beta_pheno, precision=highest, preferred_element_type=jnp.float32
    )
    pheno_sumsq = jnp.sum(pheno_resid * pheno_resid, axis=0)
    pheno_bf = pheno_resid.astype(jnp.bfloat16)
    pheno_var = pheno_sumsq / samples + 0.1
    width = 1024
    blocks = variants // width

    def one_block(index, totals):
        start = index * width
        dose_block = lax.dynamic_slice_in_dim(dose_all, start, width, 1).astype(jnp.float32)
        cov_dose = jnp.dot(
            covars_all.T, dose_block, precision=highest, preferred_element_type=jnp.float32
        )
        beta_dose = jax.scipy.linalg.cho_solve((factor, True), cov_dose)
        dose_resid = dose_block - jnp.dot(
            covars_all, beta_dose, precision=highest, preferred_element_type=jnp.float32
        )
        dose_var = jnp.sum(dose_resid * dose_resid, axis=0) / samples + 0.1
        cross = lax.dot_general(
            pheno_bf,
            dose_resid.astype(jnp.bfloat16),
            (((0,), (0,)), ((), ())),
            preferred_element_type=jnp.float32,
        )
        zscore = cross / (scale_root * jnp.sqrt(pheno_var[:, None] * dose_var[None, :]))
        chi_square = zscore * zscore
        return (
            totals[0] + jnp.sum(chi_square, axis=1),
            totals[1] + jnp.sum(jax.nn.sigmoid(2.0 * (chi_square - 4.0)), axis=1),
        )

    zeros = jnp.zeros((gene_own,), jnp.float32)
    chi_total, hit_total = lax.fori_loop(0, blocks, one_block, (zeros, zeros))
    return (chi_total / variants, 20.0 / variants * hit_total)


def solution(mesh):
    return jax.shard_map(
        local,
        mesh=mesh,
        in_specs=(
            P(("cohort", "tile"), None),
            P(("cohort", "tile"), None),
            P(("cohort", "tile"), None),
        ),
        out_specs=(P(("cohort", "tile")), P(("cohort", "tile"))),
        check_vma=False,
    )
```

profile of v0, /device:TPU:0, one launch (start us, length us, event | category | flops | bytes accessed | tf_op | source)
XLA Modules:
  0.0 117.5 jit_solution(11533161251048784845)
XLA Ops:
  7.2 0.7 all-gather.2.cloned.1.call-update
  7.9 1.0 all_to_all.14
  8.9 0.7 copy.15
  9.6 7.4 %all-to-all-start = ((f32[16,16,112]{2,0,1:T(8,128)}), f32[16,16,112]{2,0,1:T(8,128)S(1)}, u32[]{:S(2)}, u32[]{:S(2)}) async-start(f32[16,16,112]{2,0,1:T(8,128)} %copy.15), calls=%async_computation | async-start | bytes 262144 | tf_op jit(solution)/shard_map/all_to_all | solution.py:18
  17.0 22.7 %all_gather.7 = f32[256,16]{1,0:T(8,128)S(1)} all-gather(f32[16,16]{1,0:T(8,128)} %param.6), channel_id=1, replica_groups=mesh['cohort'=2,'tile'=16] {'tile'}, dimensions={0}, use_global_device_ids=true | all-gather | bytes 17408 | tf_op jit(solution)/shard_map/all_gather | solution.py:16
  39.8 0.4 fusion.20
  40.2 1.5 %cholesky.18 = f32[16,16]{1,0:T(8,128)S(1)} custom-call(f32[16,16]{1,0:T(8,128)S(1)} %fusion.19), custom_call_target="Cholesky" | custom-call | tf_op jit(solution)/shard_map/jit(cholesky)/cholesky | solution.py:20
  41.7 0.6 compare_reduce_fusion
  42.4 0.6 select_bitcast_fusion
  43.0 1.2 %custom-call.24 = f32[1,16,16]{1,2,0:T(8,128)S(1)} custom-call(f32[1,16,16]{2,1,0:T(8,128)S(1)} %get-tuple-element.272), custom_call_target="InvertDiagBlocksLowerTriangular" | custom-call | tf_op jit(solution)/shard_map/jit(_cho_solve)/triangular_solve | solution.py:24
  44.4 0.3 fusion.21
  45.1 0.4 multiply_reduce_fusion.1
  45.6 18.0 %all-gather.2.cloned.1.call-done = bf16[256,8192]{1,0:T(8,128)(2,1)} async-done(((bf16[16,8192]{1,0:T(8,128)(2,1)}), bf16[256,8192]{1,0:T(8,128)(2,1)}) %all-gather.2.cloned.1.call-update) | async-done | bytes 4194320 | tf_op jit(solution)/shard_map/all_gather | solution.py:17
  63.6 46.5 %while.18 = (s32[]{:T(128)}, f32[112]{0:T(128)S(1)}, f32[112]{0:T(128)S(1)}, bf16[256,8192]{1,0:T(8,128)(2,1)}, f32[16,16]{1,0:T(8,128)S(1)}, /*index=5*/f32[256...) while((s32[]{:T(128)}, f32[112]{0:T(128)S(1)}, ...), condition=%wide.region_7.8_spmd.clone, body=%wide.region_3.7_spmd.clone.sunk | while | flops 168249056 | bytes 2605173 | solution.py:59
  63.6 1.4 %fusion.62 = f32[1024,16]{0,1:T(8,128)S(1)} fusion(f32[256,16]{0,1:T(8,128)S(1)} %get-tuple-element.375, bf16[256,8192]{1,0:T(8,128)(2,1)} %get-tuple-element.373, s32[]{:T(128)S(6)} %select_n.19), kind=kOutput, calls=%fused_computation.7.clone.1 | convolution fusion | flops 50331648 | bytes 606212 | tf_op jit(solution)/shard_map/while/body/eval_jaxpr/dot_general | solution.py:37
  65.0 1.2 %custom-call.29 = f32[1,16,16]{1,2,0:T(8,128)S(1)} custom-call(f32[1,16,16]{2,1,0:T(8,128)S(1)} %bitcast_select_fusion.2), custom_call_target="InvertDiagBlocksLowerTriangular" | custom-call | tf_op jit(solution)/shard_map/while/body/eval_jaxpr/jit(_cho_solve)/triangular_solve | solution.py:40
  66.2 0.3 fusion.63
  66.7 2.1 %multiply_reduce_fusion.3 = (f32[1024]{0:T(1024)S(1)}, bf16[256,1024]{1,0:T(8,128)(2,1)S(1)}) fusion(f32[16,1024]{1,0:T(8,128)S(1)} %fusion.64, f32[256,16]{0,1:T(8,128)S(1)} %get-tuple-element.375, bf16[256,8192]{1,0:T(8,128)(2,1)} %get-tuple-element.373, s32[]{:T(128)S(6)} %select_n.19), kind=kOutput, calls=%fused_computation.5.clone.1 | convolution fusion | flops 51641344 | bytes 1134596 | tf_op jit(solution)/shard_map/while/body/eval_jaxpr/dot_general | solution.py:41
  68.8 0.6 fusion.65
  69.4 1.4 %fusion.62 = f32[1024,16]{0,1:T(8,128)S(1)} fusion(f32[256,16]{0,1:T(8,128)S(1)} %get-tuple-element.375, bf16[256,8192]{1,0:T(8,128)(2,1)} %get-tuple-element.373, s32[]{:T(128)S(6)} %select_n.19), kind=kOutput, calls=%fused_computation.7.clone.1 | convolution fusion | flops 50331648 | bytes 606212 | tf_op jit(solution)/shard_map/while/body/eval_jaxpr/dot_general | solution.py:37
  70.8 1.2 %custom-call.29 = f32[1,16,16]{1,2,0:T(8,128)S(1)} custom-call(f32[1,16,16]{2,1,0:T(8,128)S(1)} %bitcast_select_fusion.2), custom_call_target="InvertDiagBlocksLowerTriangular" | custom-call | tf_op jit(solution)/shard_map/while/body/eval_jaxpr/jit(_cho_solve)/triangular_solve | solution.py:40
  72.5 2.1 %multiply_reduce_fusion.3 = (f32[1024]{0:T(1024)S(1)}, bf16[256,1024]{1,0:T(8,128)(2,1)S(1)}) fusion(f32[16,1024]{1,0:T(8,128)S(1)} %fusion.64, f32[256,16]{0,1:T(8,128)S(1)} %get-tuple-element.375, bf16[256,8192]{1,0:T(8,128)(2,1)} %get-tuple-element.373, s32[]{:T(128)S(6)} %select_n.19), kind=kOutput, calls=%fused_computation.5.clone.1 | convolution fusion | flops 51641344 | bytes 1134596 | tf_op jit(solution)/shard_map/while/body/eval_jaxpr/dot_general | solution.py:41
  74.7 0.6 fusion.65
  75.2 1.4 %fusion.62 = f32[1024,16]{0,1:T(8,128)S(1)} fusion(f32[256,16]{0,1:T(8,128)S(1)} %get-tuple-element.375, bf16[256,8192]{1,0:T(8,128)(2,1)} %get-tuple-element.373, s32[]{:T(128)S(6)} %select_n.19), kind=kOutput, calls=%fused_computation.7.clone.1 | convolution fusion | flops 50331648 | bytes 606212 | tf_op jit(solution)/shard_map/while/body/eval_jaxpr/dot_general | solution.py:37
  76.6 1.2 %custom-call.29 = f32[1,16,16]{1,2,0:T(8,128)S(1)} custom-call(f32[1,16,16]{2,1,0:T(8,128)S(1)} %bitcast_select_fusion.2), custom_call_target="InvertDiagBlocksLowerTriangular" | custom-call | tf_op jit(solution)/shard_map/while/body/eval_jaxpr/jit(_cho_solve)/triangular_solve | solution.py:40
  78.3 2.1 %multiply_reduce_fusion.3 = (f32[1024]{0:T(1024)S(1)}, bf16[256,1024]{1,0:T(8,128)(2,1)S(1)}) fusion(f32[16,1024]{1,0:T(8,128)S(1)} %fusion.64, f32[256,16]{0,1:T(8,128)S(1)} %get-tuple-element.375, bf16[256,8192]{1,0:T(8,128)(2,1)} %get-tuple-element.373, s32[]{:T(128)S(6)} %select_n.19), kind=kOutput, calls=%fused_computation.5.clone.1 | convolution fusion | flops 51641344 | bytes 1134596 | tf_op jit(solution)/shard_map/while/body/eval_jaxpr/dot_general | solution.py:41
  80.5 0.6 fusion.65
  81.1 1.4 %fusion.62 = f32[1024,16]{0,1:T(8,128)S(1)} fusion(f32[256,16]{0,1:T(8,128)S(1)} %get-tuple-element.375, bf16[256,8192]{1,0:T(8,128)(2,1)} %get-tuple-element.373, s32[]{:T(128)S(6)} %select_n.19), kind=kOutput, calls=%fused_computation.7.clone.1 | convolution fusion | flops 50331648 | bytes 606212 | tf_op jit(solution)/shard_map/while/body/eval_jaxpr/dot_general | solution.py:37
  82.4 1.2 %custom-call.29 = f32[1,16,16]{1,2,0:T(8,128)S(1)} custom-call(f32[1,16,16]{2,1,0:T(8,128)S(1)} %bitcast_select_fusion.2), custom_call_target="InvertDiagBlocksLowerTriangular" | custom-call | tf_op jit(solution)/shard_map/while/body/eval_jaxpr/jit(_cho_solve)/triangular_solve | solution.py:40
  84.1 2.1 %multiply_reduce_fusion.3 = (f32[1024]{0:T(1024)S(1)}, bf16[256,1024]{1,0:T(8,128)(2,1)S(1)}) fusion(f32[16,1024]{1,0:T(8,128)S(1)} %fusion.64, f32[256,16]{0,1:T(8,128)S(1)} %get-tuple-element.375, bf16[256,8192]{1,0:T(8,128)(2,1)} %get-tuple-element.373, s32[]{:T(128)S(6)} %select_n.19), kind=kOutput, calls=%fused_computation.5.clone.1 | convolution fusion | flops 51641344 | bytes 1134596 | tf_op jit(solution)/shard_map/while/body/eval_jaxpr/dot_general | solution.py:41
  86.3 0.6 fusion.65
  86.9 1.4 %fusion.62 = f32[1024,16]{0,1:T(8,128)S(1)} fusion(f32[256,16]{0,1:T(8,128)S(1)} %get-tuple-element.375, bf16[256,8192]{1,0:T(8,128)(2,1)} %get-tuple-element.373, s32[]{:T(128)S(6)} %select_n.19), kind=kOutput, calls=%fused_computation.7.clone.1 | convolution fusion | flops 50331648 | bytes 606212 | tf_op jit(solution)/shard_map/while/body/eval_jaxpr/dot_general | solution.py:37
  88.2 1.2 %custom-call.29 = f32[1,16,16]{1,2,0:T(8,128)S(1)} custom-call(f32[1,16,16]{2,1,0:T(8,128)S(1)} %bitcast_select_fusion.2), custom_call_target="InvertDiagBlocksLowerTriangular" | custom-call | tf_op jit(solution)/shard_map/while/body/eval_jaxpr/jit(_cho_solve)/triangular_solve | solution.py:40
  90.0 2.1 %multiply_reduce_fusion.3 = (f32[1024]{0:T(1024)S(1)}, bf16[256,1024]{1,0:T(8,128)(2,1)S(1)}) fusion(f32[16,1024]{1,0:T(8,128)S(1)} %fusion.64, f32[256,16]{0,1:T(8,128)S(1)} %get-tuple-element.375, bf16[256,8192]{1,0:T(8,128)(2,1)} %get-tuple-element.373, s32[]{:T(128)S(6)} %select_n.19), kind=kOutput, calls=%fused_computation.5.clone.1 | convolution fusion | flops 51641344 | bytes 1134596 | tf_op jit(solution)/shard_map/while/body/eval_jaxpr/dot_general | solution.py:41
  92.1 0.6 fusion.65
  92.7 1.4 %fusion.62 = f32[1024,16]{0,1:T(8,128)S(1)} fusion(f32[256,16]{0,1:T(8,128)S(1)} %get-tuple-element.375, bf16[256,8192]{1,0:T(8,128)(2,1)} %get-tuple-element.373, s32[]{:T(128)S(6)} %select_n.19), kind=kOutput, calls=%fused_computation.7.clone.1 | convolution fusion | flops 50331648 | bytes 606212 | tf_op jit(solution)/shard_map/while/body/eval_jaxpr/dot_general | solution.py:37
  94.1 1.2 %custom-call.29 = f32[1,16,16]{1,2,0:T(8,128)S(1)} custom-call(f32[1,16,16]{2,1,0:T(8,128)S(1)} %bitcast_select_fusion.2), custom_call_target="InvertDiagBlocksLowerTriangular" | custom-call | tf_op jit(solution)/shard_map/while/body/eval_jaxpr/jit(_cho_solve)/triangular_solve | solution.py:40
  95.8 2.1 %multiply_reduce_fusion.3 = (f32[1024]{0:T(1024)S(1)}, bf16[256,1024]{1,0:T(8,128)(2,1)S(1)}) fusion(f32[16,1024]{1,0:T(8,128)S(1)} %fusion.64, f32[256,16]{0,1:T(8,128)S(1)} %get-tuple-element.375, bf16[256,8192]{1,0:T(8,128)(2,1)} %get-tuple-element.373, s32[]{:T(128)S(6)} %select_n.19), kind=kOutput, calls=%fused_computation.5.clone.1 | convolution fusion | flops 51641344 | bytes 1134596 | tf_op jit(solution)/shard_map/while/body/eval_jaxpr/dot_general | solution.py:41
  97.9 0.6 fusion.65
  98.5 1.4 %fusion.62 = f32[1024,16]{0,1:T(8,128)S(1)} fusion(f32[256,16]{0,1:T(8,128)S(1)} %get-tuple-element.375, bf16[256,8192]{1,0:T(8,128)(2,1)} %get-tuple-element.373, s32[]{:T(128)S(6)} %select_n.19), kind=kOutput, calls=%fused_computation.7.clone.1 | convolution fusion | flops 50331648 | bytes 606212 | tf_op jit(solution)/shard_map/while/body/eval_jaxpr/dot_general | solution.py:37
  99.9 1.2 %custom-call.29 = f32[1,16,16]{1,2,0:T(8,128)S(1)} custom-call(f32[1,16,16]{2,1,0:T(8,128)S(1)} %bitcast_select_fusion.2), custom_call_target="InvertDiagBlocksLowerTriangular" | custom-call | tf_op jit(solution)/shard_map/while/body/eval_jaxpr/jit(_cho_solve)/triangular_solve | solution.py:40
  101.6 2.1 %multiply_reduce_fusion.3 = (f32[1024]{0:T(1024)S(1)}, bf16[256,1024]{1,0:T(8,128)(2,1)S(1)}) fusion(f32[16,1024]{1,0:T(8,128)S(1)} %fusion.64, f32[256,16]{0,1:T(8,128)S(1)} %get-tuple-element.375, bf16[256,8192]{1,0:T(8,128)(2,1)} %get-tuple-element.373, s32[]{:T(128)S(6)} %select_n.19), kind=kOutput, calls=%fused_computation.5.clone.1 | convolution fusion | flops 51641344 | bytes 1134596 | tf_op jit(solution)/shard_map/while/body/eval_jaxpr/dot_general | solution.py:41
  103.7 0.6 fusion.65
  104.3 1.4 %fusion.62 = f32[1024,16]{0,1:T(8,128)S(1)} fusion(f32[256,16]{0,1:T(8,128)S(1)} %get-tuple-element.375, bf16[256,8192]{1,0:T(8,128)(2,1)} %get-tuple-element.373, s32[]{:T(128)S(6)} %select_n.19), kind=kOutput, calls=%fused_computation.7.clone.1 | convolution fusion | flops 50331648 | bytes 606212 | tf_op jit(solution)/shard_map/while/body/eval_jaxpr/dot_general | solution.py:37
  105.7 1.2 %custom-call.29 = f32[1,16,16]{1,2,0:T(8,128)S(1)} custom-call(f32[1,16,16]{2,1,0:T(8,128)S(1)} %bitcast_select_fusion.2), custom_call_target="InvertDiagBlocksLowerTriangular" | custom-call | tf_op jit(solution)/shard_map/while/body/eval_jaxpr/jit(_cho_solve)/triangular_solve | solution.py:40
  107.4 2.1 %multiply_reduce_fusion.3 = (f32[1024]{0:T(1024)S(1)}, bf16[256,1024]{1,0:T(8,128)(2,1)S(1)}) fusion(f32[16,1024]{1,0:T(8,128)S(1)} %fusion.64, f32[256,16]{0,1:T(8,128)S(1)} %get-tuple-element.375, bf16[256,8192]{1,0:T(8,128)(2,1)} %get-tuple-element.373, s32[]{:T(128)S(6)} %select_n.19), kind=kOutput, calls=%fused_computation.5.clone.1 | convolution fusion | flops 51641344 | bytes 1134596 | tf_op jit(solution)/shard_map/while/body/eval_jaxpr/dot_general | solution.py:41
  109.5 0.6 fusion.65
  110.1 0.5 broadcast_multiply_fusion
  (52 shorter events, 4.4 us)
Async XLA Ops:
  7.2 56.5 %all-gather.2.cloned.1.call-start = ((), (), s32[]{:S(2)}) async-start(), calls=%async_computation.1 | async-start | bytes 4456448 | tf_op jit(solution)/shard_map/all_gather | solution.py:17
  9.6 34.7 %all-to-all-start = ((f32[16,16,112]{2,0,1:T(8,128)}), f32[16,16,112]{2,0,1:T(8,128)S(1)}, u32[]{:S(2)}, u32[]{:S(2)}) async-start(f32[16,16,112]{2,0,1:T(8,128)} %copy.15), calls=%async_computation | async-start | bytes 262144 | tf_op jit(solution)/shard_map/all_to_all | solution.py:18
Sparse Core Ops, SparseCore 0:
  10.1 53.4 all-gather.1
where the time goes:
time: 118 us; the launch traced here: 117 us
  matrix products  37.4 us (32%)
  blocking collectives  22.7 us (19%)
  waiting for transfers between devices  18.7 us (16%)
  other arithmetic  14.6 us (12%)
  between operations  14.1 us (12%)
  starting transfers between devices  7.45 us (6%)
  local copies, waits for them, and re-layouts  2.05 us (2%)
    all_gather x1, blocking collectives, local(): covars_all = lax.all_gather(covars, 'tile', axis=0, tiled=True)  22.7 us
    all_gather x1, waiting for transfers between devices, local(): dose_all = lax.all_gather(dosage, 'tile', axis=0, tiled=True)  18 us
    dot_general x8, matrix products, one_block(): jnp.dot(covars_all, beta_dose, precision=highest, preferred_element_type=...  17 us
    dot_general x8, matrix products, one_block(): jnp.dot(covars_all.T, dose_block, precision=highest, preferred_element_ty...  10.9 us
    another operation x16, other arithmetic, one_block(): beta_dose = jax.scipy.linalg.cho_solve((factor, True), cov_dose)  9.88 us
    all_to_all x1, starting transfers between devices, local(): lax.all_to_all(phenotypes, 'tile', split_axis=1, concat_axis=0, tiled=True)  7.41 us
    dot_general x8, matrix products, one_block(): lax.dot_general(pheno_bf, dose_resid.astype(jnp.bfloat16), (((0,), (0,)),...  4.42 us
    another operation x16, matrix products, one_block(): beta_dose = jax.scipy.linalg.cho_solve((factor, True), cov_dose)  3.7 us
  transfers between devices with their start and end apart: 2, of which 1 were waited for; matrix products, arithmetic and copies ran while one was open for 6% of the time, Pallas kernels for 0%

commit v1 on v0

--- a/solution.py
+++ b/solution.py
@@ -13,8 +13,11 @@
     genes_all = phenotypes.shape[1]
     gene_own = genes_all // devices
     scale_root = jnp.sqrt(jnp.float32(samples))
-    covars_all = lax.all_gather(covars, "tile", axis=0, tiled=True)
-    dose_all = lax.all_gather(dosage, "tile", axis=0, tiled=True)
+    covars_all, dose_all = jnp.split(
+        lax.all_gather(jnp.concatenate([covars, dosage], axis=1), "tile", axis=0, tiled=True),
+        [covars.shape[1]],
+        axis=1,
+    )
     pheno_own = lax.all_to_all(phenotypes, "tile", split_axis=1, concat_axis=0, tiled=True)
     gram = jnp.dot(covars_all.T, covars_all, precision=highest, preferred_element_type=jnp.float32)
     factor = jnp.linalg.cholesky(gram)

time: 118 us -> 168 us (1.42)
  waiting for transfers between devices: 18.7 us -> 69.8 us
  blocking collectives: 22.7 us -> 0 us
  local copies, waits for them, and re-layouts: 2.05 us -> 11.8 us
  matrix products: 37.4 us -> 45.6 us
  other arithmetic: 14.6 us -> 17.3 us
    all_gather x1, waiting for transfers between devices: 18 us -> 61.7 us  [local(): lax.all_gather(jnp.concatenate([covars, dosage], axis=1), 'tile', axis=0,...]
    all_gather x1 -> x0, blocking collectives: 22.7 us -> none  [local(): covars_all = lax.all_gather(covars, 'tile', axis=0, tiled=True)]
    split x0 -> x2, local copies, waits for them, and re-layouts: none -> 9.79 us  [local(): jnp.split(lax.all_gather(jnp.concatenate([covars, dosage], axis=1), 'tile...]
    all_to_all x1, waiting for transfers between devices: 0.01 us -> 8.06 us  [local(): lax.all_to_all(phenotypes, 'tile', split_axis=1, concat_axis=0, tiled=True)]
    dot_general x8, matrix products: 10.9 us -> 15 us  [one_block(): jnp.dot(covars_all.T, dose_block, precision=highest, preferred_element_ty...]
    concatenate x0 -> x1, other arithmetic: none -> 1.74 us  [local(): jnp.concatenate([covars, dosage], axis=1)]
  transfers between devices with their start and end apart: 2 -> 2, of which waited for: 1 -> 2; matrix products, arithmetic and copies ran while one was open for 6% -> 0% of each run, Pallas kernels for 0% -> 0%
where the time goes in v1:
time: 168 us; the launch traced here: 167 us
  waiting for transfers between devices  69.8 us (42%)
  matrix products  45.6 us (27%)
  other arithmetic  17.3 us (10%)
  between operations  14.1 us (8%)
  local copies, waits for them, and re-layouts  11.8 us (7%)
  starting transfers between devices  7.45 us (4%)
    all_gather x1, waiting for transfers between devices, local(): lax.all_gather(jnp.concatenate([covars, dosage], axis=1), 'tile', axis=0,...  61.7 us
    dot_general x8, matrix products, one_block(): jnp.dot(covars_all, beta_dose, precision=highest, preferred_element_type=...  18.3 us
    dot_general x8, matrix products, one_block(): jnp.dot(covars_all.T, dose_block, precision=highest, preferred_element_ty...  15 us
    another operation x16, other arithmetic, one_block(): beta_dose = jax.scipy.linalg.cho_solve((factor, True), cov_dose)  9.88 us
    split x2, local copies, waits for them, and re-layouts, local(): jnp.split(lax.all_gather(jnp.concatenate([covars, dosage], axis=1), 'tile...  9.79 us
    all_to_all x1, waiting for transfers between devices, local(): lax.all_to_all(phenotypes, 'tile', split_axis=1, concat_axis=0, tiled=True)  8.06 us
    all_to_all x1, starting transfers between devices, local(): lax.all_to_all(phenotypes, 'tile', split_axis=1, concat_axis=0, tiled=True)  7.41 us
    dot_general x8, matrix products, one_block(): lax.dot_general(pheno_bf, dose_resid.astype(jnp.bfloat16), (((0,), (0,)),...  4.43 us
  transfers between devices with their start and end apart: 2, of which 2 were waited for; matrix products, arithmetic and copies ran while one was open for 0% of the time, Pallas kernels for 0%

profile of v1, /device:TPU:0, one launch (start us, length us, event | category | flops | bytes accessed | tf_op | source)
XLA Modules:
  0.0 166.7 jit_solution(1436347254316864222)
XLA Ops:
  7.2 1.0 convert_element_type.16
  8.2 1.7 %pad_maximum_fusion = f32[16,8208]{1,0:T(8,128)} fusion(f32[16,8192]{1,0:T(8,128)S(1)} %convert_element_type.16, f32[16,16]{1,0:T(8,128)} %param.6), kind=kLoop, calls=%fused_computation.24 | loop fusion | flops 131328 | bytes 1050624 | tf_op jit(solution)/shard_map/concatenate | solution.py:17
  10.0 1.0 all_to_all.14
  11.0 0.7 copy.19
  11.7 7.4 %all-to-all-start = ((f32[16,16,112]{2,0,1:T(8,128)}), f32[16,16,112]{2,0,1:T(8,128)S(1)}, u32[]{:S(2)}, u32[]{:S(2)}) async-start(f32[16,16,112]{2,0,1:T(8,128)} %copy.19), calls=%async_computation | async-start | bytes 262144 | tf_op jit(solution)/shard_map/all_to_all | solution.py:21
  19.1 8.1 %all-to-all-done = f32[16,16,112]{2,0,1:T(8,128)S(1)} async-done(((f32[16,16,112]{2,0,1:T(8,128)}), f32[16,16,112]{2,0,1:T(8,128)S(1)}, u32[]{:S(2)}, u32[]{:S(2)}) %all-to-all-start) | async-done | bytes 114720 | tf_op jit(solution)/shard_map/all_to_all | solution.py:21
  27.3 61.7 %all-gather.2.cloned.1.call-done = f32[256,8208]{1,0:T(8,128)} async-done(((f32[16,8208]{1,0:T(8,128)}), f32[256,8208]{1,0:T(8,128)}) %all-gather.2.cloned.1.call-update) | async-done | bytes 8405008 | tf_op jit(solution)/shard_map/all_gather | solution.py:17
  89.0 1.3 fusion.22
  90.4 1.5 cholesky.18
  91.9 0.6 compare_reduce_fusion
  92.6 0.6 select_bitcast_fusion
  93.2 1.2 custom-call.24
  94.5 1.3 fusion.20
  96.1 1.3 multiply_reduce_fusion.1
  97.5 0.9 split.9
  98.5 8.9 %split.8 = f32[256,8192]{1,0:T(8,128)} slice(f32[256,8208]{1,0:T(8,128)} %all-gather.2.cloned.1.call-done), slice={[0:256], [16:8208]} | slice | bytes 16777216 | tf_op jit(solution)/shard_map/split | solution.py:16
  107.4 51.9 %while.18 = (s32[]{:T(128)}, f32[112]{0:T(128)S(1)}, f32[112]{0:T(128)S(1)}, f32[256,8192]{1,0:T(8,128)}, f32[16,16]{1,0:T(8,128)S(1)}, /*index=5*/f32[256,16]{0...) while((s32[]{:T(128)}, f32[112]{0:T(128)S(1)}, ...), condition=%wide.region_7.8_spmd.clone, body=%wide.region_3.7_spmd.clone.sunk | while | flops 167986912 | bytes 3653749 | solution.py:62
  107.4 1.9 %fusion.60 = f32[1024,16]{0,1:T(8,128)S(1)} fusion(f32[256,16]{0,1:T(8,128)S(1)} %get-tuple-element.375, f32[256,8192]{1,0:T(8,128)} %get-tuple-element.373, s32[]{:T(128)S(6)} %select_n.19), kind=kOutput, calls=%fused_computation.6.clone.1 | convolution fusion | flops 50331648 | bytes 1130500 | tf_op jit(solution)/shard_map/while/body/eval_jaxpr/dot_general | solution.py:40
  109.3 1.2 custom-call.29
  111.0 2.3 %multiply_reduce_fusion.3 = (f32[1024]{0:T(1024)S(1)}, bf16[256,1024]{1,0:T(8,128)(2,1)S(1)}) fusion(f32[16,1024]{1,0:T(8,128)S(1)} %fusion.62, f32[256,16]{0,1:T(8,128)S(1)} %get-tuple-element.375, f32[256,8192]{1,0:T(8,128)} %get-tuple-element.373, s32[]{:T(128)S(6)} %select_n.19), kind=kOutput, calls=%fused_computation.5.clone.1 | convolution fusion | flops 51379200 | bytes 1658884 | tf_op jit(solution)/shard_map/while/body/eval_jaxpr/dot_general | solution.py:44
  113.3 0.6 fusion.63
  113.9 1.9 %fusion.60 = f32[1024,16]{0,1:T(8,128)S(1)} fusion(f32[256,16]{0,1:T(8,128)S(1)} %get-tuple-element.375, f32[256,8192]{1,0:T(8,128)} %get-tuple-element.373, s32[]{:T(128)S(6)} %select_n.19), kind=kOutput, calls=%fused_computation.6.clone.1 | convolution fusion | flops 50331648 | bytes 1130500 | tf_op jit(solution)/shard_map/while/body/eval_jaxpr/dot_general | solution.py:40
  115.8 1.2 custom-call.29
  117.5 2.3 %multiply_reduce_fusion.3 = (f32[1024]{0:T(1024)S(1)}, bf16[256,1024]{1,0:T(8,128)(2,1)S(1)}) fusion(f32[16,1024]{1,0:T(8,128)S(1)} %fusion.62, f32[256,16]{0,1:T(8,128)S(1)} %get-tuple-element.375, f32[256,8192]{1,0:T(8,128)} %get-tuple-element.373, s32[]{:T(128)S(6)} %select_n.19), kind=kOutput, calls=%fused_computation.5.clone.1 | convolution fusion | flops 51379200 | bytes 1658884 | tf_op jit(solution)/shard_map/while/body/eval_jaxpr/dot_general | solution.py:44
  119.8 0.6 fusion.63
  120.4 1.9 %fusion.60 = f32[1024,16]{0,1:T(8,128)S(1)} fusion(f32[256,16]{0,1:T(8,128)S(1)} %get-tuple-element.375, f32[256,8192]{1,0:T(8,128)} %get-tuple-element.373, s32[]{:T(128)S(6)} %select_n.19), kind=kOutput, calls=%fused_computation.6.clone.1 | convolution fusion | flops 50331648 | bytes 1130500 | tf_op jit(solution)/shard_map/while/body/eval_jaxpr/dot_general | solution.py:40
  122.3 1.2 custom-call.29
  124.0 2.3 %multiply_reduce_fusion.3 = (f32[1024]{0:T(1024)S(1)}, bf16[256,1024]{1,0:T(8,128)(2,1)S(1)}) fusion(f32[16,1024]{1,0:T(8,128)S(1)} %fusion.62, f32[256,16]{0,1:T(8,128)S(1)} %get-tuple-element.375, f32[256,8192]{1,0:T(8,128)} %get-tuple-element.373, s32[]{:T(128)S(6)} %select_n.19), kind=kOutput, calls=%fused_computation.5.clone.1 | convolution fusion | flops 51379200 | bytes 1658884 | tf_op jit(solution)/shard_map/while/body/eval_jaxpr/dot_general | solution.py:44
  126.3 0.6 fusion.63
  126.8 1.9 %fusion.60 = f32[1024,16]{0,1:T(8,128)S(1)} fusion(f32[256,16]{0,1:T(8,128)S(1)} %get-tuple-element.375, f32[256,8192]{1,0:T(8,128)} %get-tuple-element.373, s32[]{:T(128)S(6)} %select_n.19), kind=kOutput, calls=%fused_computation.6.clone.1 | convolution fusion | flops 50331648 | bytes 1130500 | tf_op jit(solution)/shard_map/while/body/eval_jaxpr/dot_general | solution.py:40
  128.7 1.2 custom-call.29
  130.4 2.3 %multiply_reduce_fusion.3 = (f32[1024]{0:T(1024)S(1)}, bf16[256,1024]{1,0:T(8,128)(2,1)S(1)}) fusion(f32[16,1024]{1,0:T(8,128)S(1)} %fusion.62, f32[256,16]{0,1:T(8,128)S(1)} %get-tuple-element.375, f32[256,8192]{1,0:T(8,128)} %get-tuple-element.373, s32[]{:T(128)S(6)} %select_n.19), kind=kOutput, calls=%fused_computation.5.clone.1 | convolution fusion | flops 51379200 | bytes 1658884 | tf_op jit(solution)/shard_map/while/body/eval_jaxpr/dot_general | solution.py:44
  132.8 0.6 fusion.63
  133.3 1.9 %fusion.60 = f32[1024,16]{0,1:T(8,128)S(1)} fusion(f32[256,16]{0,1:T(8,128)S(1)} %get-tuple-element.375, f32[256,8192]{1,0:T(8,128)} %get-tuple-element.373, s32[]{:T(128)S(6)} %select_n.19), kind=kOutput, calls=%fused_computation.6.clone.1 | convolution fusion | flops 50331648 | bytes 1130500 | tf_op jit(solution)/shard_map/while/body/eval_jaxpr/dot_general | solution.py:40
  135.2 1.2 custom-call.29
  136.9 2.3 %multiply_reduce_fusion.3 = (f32[1024]{0:T(1024)S(1)}, bf16[256,1024]{1,0:T(8,128)(2,1)S(1)}) fusion(f32[16,1024]{1,0:T(8,128)S(1)} %fusion.62, f32[256,16]{0,1:T(8,128)S(1)} %get-tuple-element.375, f32[256,8192]{1,0:T(8,128)} %get-tuple-element.373, s32[]{:T(128)S(6)} %select_n.19), kind=kOutput, calls=%fused_computation.5.clone.1 | convolution fusion | flops 51379200 | bytes 1658884 | tf_op jit(solution)/shard_map/while/body/eval_jaxpr/dot_general | solution.py:44
  139.2 0.6 fusion.63
  139.8 1.9 %fusion.60 = f32[1024,16]{0,1:T(8,128)S(1)} fusion(f32[256,16]{0,1:T(8,128)S(1)} %get-tuple-element.375, f32[256,8192]{1,0:T(8,128)} %get-tuple-element.373, s32[]{:T(128)S(6)} %select_n.19), kind=kOutput, calls=%fused_computation.6.clone.1 | convolution fusion | flops 50331648 | bytes 1130500 | tf_op jit(solution)/shard_map/while/body/eval_jaxpr/dot_general | solution.py:40
  141.7 1.2 custom-call.29
  143.4 2.3 %multiply_reduce_fusion.3 = (f32[1024]{0:T(1024)S(1)}, bf16[256,1024]{1,0:T(8,128)(2,1)S(1)}) fusion(f32[16,1024]{1,0:T(8,128)S(1)} %fusion.62, f32[256,16]{0,1:T(8,128)S(1)} %get-tuple-element.375, f32[256,8192]{1,0:T(8,128)} %get-tuple-element.373, s32[]{:T(128)S(6)} %select_n.19), kind=kOutput, calls=%fused_computation.5.clone.1 | convolution fusion | flops 51379200 | bytes 1658884 | tf_op jit(solution)/shard_map/while/body/eval_jaxpr/dot_general | solution.py:44
  145.7 0.6 fusion.63
  146.3 1.9 %fusion.60 = f32[1024,16]{0,1:T(8,128)S(1)} fusion(f32[256,16]{0,1:T(8,128)S(1)} %get-tuple-element.375, f32[256,8192]{1,0:T(8,128)} %get-tuple-element.373, s32[]{:T(128)S(6)} %select_n.19), kind=kOutput, calls=%fused_computation.6.clone.1 | convolution fusion | flops 50331648 | bytes 1130500 | tf_op jit(solution)/shard_map/while/body/eval_jaxpr/dot_general | solution.py:40
  148.2 1.2 custom-call.29
  149.9 2.3 %multiply_reduce_fusion.3 = (f32[1024]{0:T(1024)S(1)}, bf16[256,1024]{1,0:T(8,128)(2,1)S(1)}) fusion(f32[16,1024]{1,0:T(8,128)S(1)} %fusion.62, f32[256,16]{0,1:T(8,128)S(1)} %get-tuple-element.375, f32[256,8192]{1,0:T(8,128)} %get-tuple-element.373, s32[]{:T(128)S(6)} %select_n.19), kind=kOutput, calls=%fused_computation.5.clone.1 | convolution fusion | flops 51379200 | bytes 1658884 | tf_op jit(solution)/shard_map/while/body/eval_jaxpr/dot_general | solution.py:44
  152.2 0.6 fusion.63
  152.8 1.9 %fusion.60 = f32[1024,16]{0,1:T(8,128)S(1)} fusion(f32[256,16]{0,1:T(8,128)S(1)} %get-tuple-element.375, f32[256,8192]{1,0:T(8,128)} %get-tuple-element.373, s32[]{:T(128)S(6)} %select_n.19), kind=kOutput, calls=%fused_computation.6.clone.1 | convolution fusion | flops 50331648 | bytes 1130500 | tf_op jit(solution)/shard_map/while/body/eval_jaxpr/dot_general | solution.py:40
  154.7 1.2 custom-call.29
  156.4 2.3 %multiply_reduce_fusion.3 = (f32[1024]{0:T(1024)S(1)}, bf16[256,1024]{1,0:T(8,128)(2,1)S(1)}) fusion(f32[16,1024]{1,0:T(8,128)S(1)} %fusion.62, f32[256,16]{0,1:T(8,128)S(1)} %get-tuple-element.375, f32[256,8192]{1,0:T(8,128)} %get-tuple-element.373, s32[]{:T(128)S(6)} %select_n.19), kind=kOutput, calls=%fused_computation.5.clone.1 | convolution fusion | flops 51379200 | bytes 1658884 | tf_op jit(solution)/shard_map/while/body/eval_jaxpr/dot_general | solution.py:44
  (55 shorter events, 5.8 us)
Async XLA Ops:
  7.2 81.9 %all-gather.2.cloned.1.call-start = ((), (), s32[]{:S(2)}) async-start(), calls=%async_computation.1 | async-start | bytes 9052160 | tf_op jit(solution)/shard_map/all_gather | solution.py:17
  11.7 15.5 %all-to-all-start = ((f32[16,16,112]{2,0,1:T(8,128)}), f32[16,16,112]{2,0,1:T(8,128)S(1)}, u32[]{:S(2)}, u32[]{:S(2)}) async-start(f32[16,16,112]{2,0,1:T(8,128)} %copy.19), calls=%async_computation | async-start | bytes 262144 | tf_op jit(solution)/shard_map/all_to_all | solution.py:21
Sparse Core Ops, SparseCore 0:
  10.3 78.7 all-gather.1
